TPU v7x, 32 devices: a whole 2x2x4 slice. The times are simulated.
32 devices in a mesh: dp: 8 (over y, x, core), mp: 4 (over z).
Axes of the slice: x: 2, y: 2, z: 4, core: 2. Of those that a mesh axis runs over, the one named last changes fastest.
Arguments:
- hidden: bfloat16 [64, 4096], P('dp'), may hold values from -6 to 6
- attention_gain: float32 [4096], replicated, may hold values from 0.5 to 1.5
- query_weight: bfloat16 [4096, 4096], P(None, 'mp'), may hold values from -0.09375 to 0.09375
- key_weight: bfloat16 [4096, 1024], P(None, 'mp'), may hold values from -0.09375 to 0.09375
- value_weight: bfloat16 [4096, 1024], P(None, 'mp'), may hold values from -0.09375 to 0.09375
- output_weight: bfloat16 [4096, 4096], P('mp'), may hold values from -0.09375 to 0.09375
- key_cache: bfloat16 [64, 8, 4096, 128], P('dp', 'mp'), may hold values from -9 to 9
- value_cache: bfloat16 [64, 8, 4096, 128], P('dp', 'mp'), may hold values from -8 to 8, as said below
- lengths: int32 [64], P('dp'), may hold values from 128 to 4096, as said below
- finished: int32 [64], P('dp'), may hold values 0 or 1
- feed_gain: float32 [4096], replicated, may hold values from 0.5 to 1.5
- gate_weight: bfloat16 [4096, 14336], P(None, ('dp', 'mp')), may hold values from -0.09375 to 0.09375
- up_weight: bfloat16 [4096, 14336], P(None, ('dp', 'mp')), may hold values from -0.09375 to 0.09375
- down_weight: bfloat16 [14336, 4096], P(('dp', 'mp')), may hold values from -0.046875 to 0.046875
- final_gain: float32 [4096], replicated, may hold values from 0.5 to 8, as said below
- vocab_weight: bfloat16 [4096, 128256], P(None, ('dp', 'mp')), may hold values from -0.375 to 0.375
- next_tokens: int32 [64], replicated, may hold values from 0 to 128255
Outputs:
- log_likelihood: float32 [64], P('dp')
Inputs may be any that keep to these rules, and one draw needn't show every extreme that they name: `lengths`: each rollout has 128 to 4096 cached tokens; both ends are reached in every draw; rollouts held by one index of dp share a length scale, so devices' total cached tokens differ. `finished`: 0 or 1. `next_tokens`: a vocabulary entry. `value_cache`: a per-rollout and per-head mean plus noise. `final_gain`: positive gains.
All inputs are finite; a program needn't handle non-finite values.
Results may differ from a plain program's by a relative error of at most 0.0055.
Values may be sent and summed in bfloat16 or wider, within the bound.
A program may use at most 192 MiB of HBM per device.

v0:
```python
import math

import jax
import jax.numpy as jnp
from jax import lax
from jax.sharding import PartitionSpec as P

H = 32
KVH = 8


EPSILON = 1e-05
THETA = 500000.0
NEGATIVE = -1e30


def joined(value, axis, join):
    pieces = jax.tree.map(lambda part: lax.all_gather(part, axis), value)
    head = jax.tree.map(lambda part: part[0], pieces)
    tail = jax.tree.map(lambda part: part[1:], pieces)
    subtotal, _ = lax.scan(lambda subtotal, piece: (join(subtotal, piece), None), head, tail)
    return subtotal


def rms_norm(hidden, gain):
    wide = hidden.astype(jnp.float32)
    scale = lax.rsqrt(jnp.mean(wide * wide, axis=-1, keepdims=True) + EPSILON)
    return (wide * scale * gain).astype(jnp.bfloat16)


def rotate(heads, positions):
    half = heads.shape[-1] // 2
    exponent = jnp.arange(half, dtype=jnp.float32) * (-2.0 / heads.shape[-1])
    frequency = jnp.power(jnp.float32(THETA), exponent)
    angles = positions.astype(jnp.float32)[:, None, None] * frequency[None, None, :]
    cosine = jnp.cos(angles)
    sine = jnp.sin(angles)
    former = heads[..., :half]
    latter = heads[..., half:]
    return jnp.concatenate(
        [former * cosine - latter * sine, latter * cosine + former * sine], axis=-1
    )


def combine_parts(former, latter):
    highest = jnp.maximum(former[0], latter[0])
    spread = former[1] * jnp.exp(former[0] - highest) + latter[1] * jnp.exp(latter[0] - highest)
    return (highest, spread, former[2] + latter[2])


def padded_attention(queries, own, key_cache, value_cache, new_values, lengths):
    head_width = queries.shape[-1]
    scale = 1.0 / math.sqrt(head_width)
    scores = (
        jnp.einsum("rkgd,rkld->rkgl", queries, key_cache, preferred_element_type=jnp.float32)
        * scale
    )
    places = lax.broadcasted_iota(jnp.int32, (1, 1, 1, key_cache.shape[2]), 3)
    scores = jnp.where(places < lengths[:, None, None, None], scores, NEGATIVE)
    top = jnp.maximum(jnp.max(scores, axis=-1), own)
    weights = jnp.exp(scores - top[..., None])
    own_weight = jnp.exp(own - top)
    total = jnp.sum(weights, axis=-1) + own_weight
    mixed = jnp.einsum(
        "rkgl,rkld->rkgd",
        weights.astype(jnp.bfloat16),
        value_cache,
        preferred_element_type=jnp.float32,
    )
    mixed = mixed + own_weight[..., None] * new_values.astype(jnp.float32)[:, :, None, :]
    return (mixed / total[..., None]).astype(jnp.bfloat16)


def shards(
    hidden,
    attention_gain,
    query_weight,
    key_weight,
    value_weight,
    output_weight,
    key_cache,
    value_cache,
    lengths,
    finished,
    feed_gain,
    gate_weight,
    up_weight,
    down_weight,
    final_gain,
    vocab_weight,
    next_tokens,
):
    local_rows = hidden.shape[0]
    key_heads = key_cache.shape[1]
    head_width = key_cache.shape[3]
    groups = H // KVH
    normed = rms_norm(hidden, attention_gain)
    queries = jnp.dot(normed, query_weight, preferred_element_type=jnp.float32).reshape(
        local_rows, key_heads * groups, head_width
    )
    queries = (
        rotate(queries, lengths)
        .astype(jnp.bfloat16)
        .reshape(local_rows, key_heads, groups, head_width)
    )
    new_keys = jnp.dot(normed, key_weight, preferred_element_type=jnp.float32).reshape(
        local_rows, key_heads, head_width
    )
    new_keys = rotate(new_keys, lengths).astype(jnp.bfloat16)
    new_values = (
        jnp.dot(normed, value_weight, preferred_element_type=jnp.float32)
        .astype(jnp.bfloat16)
        .reshape(local_rows, key_heads, head_width)
    )
    own = jnp.einsum("rkgd,rkd->rkg", queries, new_keys, preferred_element_type=jnp.float32) * (
        1.0 / math.sqrt(head_width)
    )
    attended = padded_attention(queries, own, key_cache, value_cache, new_values, lengths)
    partial_heads = jnp.dot(
        attended.reshape(local_rows, key_heads * groups * head_width),
        output_weight,
        preferred_element_type=jnp.float32,
    )
    attention = lax.psum(partial_heads.astype(jnp.bfloat16), "mp").astype(jnp.float32)
    mixed_hidden = (hidden.astype(jnp.float32) + attention).astype(jnp.bfloat16)
    feed_in = rms_norm(mixed_hidden, feed_gain)

    def activate(piece):
        gate = jnp.dot(piece, gate_weight, preferred_element_type=jnp.float32)
        upward = jnp.dot(piece, up_weight, preferred_element_type=jnp.float32)
        return (jax.nn.silu(gate) * upward).astype(jnp.bfloat16)

    activation = activate(lax.all_gather(feed_in, "dp", axis=0, tiled=True))
    partial_feed = lax.psum_scatter(
        jnp.dot(
            lax.slice_in_dim(activation, 0, local_rows * lax.axis_size("dp"), axis=0),
            down_weight,
            preferred_element_type=jnp.float32,
        ).astype(jnp.bfloat16),
        "dp",
        scatter_dimension=0,
        tiled=True,
    ).astype(jnp.float32)
    feed = lax.psum(partial_feed.astype(jnp.bfloat16), "mp").astype(jnp.float32)
    residual = (mixed_hidden.astype(jnp.float32) + feed).astype(jnp.bfloat16)
    final = rms_norm(residual, final_gain)

    def score_rows(piece):
        return jnp.dot(piece, vocab_weight, preferred_element_type=jnp.float32)

    logits = score_rows(lax.all_gather(final, "dp", axis=0, tiled=True))
    vocab_local = vocab_weight.shape[1]
    vocab_start = (lax.axis_index("dp") * lax.axis_size("mp") + lax.axis_index("mp")) * vocab_local
    offsets = next_tokens - vocab_start
    matches = lax.broadcasted_iota(jnp.int32, (1, vocab_local), 1) == offsets[:, None]
    picked = jnp.sum(jnp.where(matches, logits, 0.0), axis=-1)
    local_top = jnp.max(logits, axis=-1)
    local_spread = jnp.sum(jnp.exp(logits - local_top[:, None]), axis=-1)
    top, spread_sum, picked = joined((local_top, local_spread, picked), ("dp", "mp"), combine_parts)
    normalizer = top + jnp.log(spread_sum)
    row_start = lax.axis_index("dp") * local_rows
    chosen = lax.dynamic_slice_in_dim(picked - normalizer, row_start, local_rows, 0)
    return jnp.where(finished != 0, 0.0, chosen).astype(jnp.float32)


def solution(mesh):
    in_specs = (
        P("dp", None),
        P(),
        P(None, "mp"),
        P(None, "mp"),
        P(None, "mp"),
        P("mp", None),
        P("dp", "mp", None, None),
        P("dp", "mp", None, None),
        P("dp"),
        P("dp"),
        P(),
        P(None, ("dp", "mp")),
        P(None, ("dp", "mp")),
        P(("dp", "mp"), None),
        P(),
        P(None, ("dp", "mp")),
        P(),
    )
    out_specs = P("dp")
    return jax.shard_map(shards, mesh=mesh, in_specs=in_specs, out_specs=out_specs, check_vma=False)
```

profile of v0, /device:TPU:0, one launch (start us, length us, event | category | flops | bytes accessed | tf_op | source)
XLA Modules:
  0.0 245.6 jit_solution(16923036715946141250)
XLA Ops:
  6.6 0.8 convert_element_type.71
  7.4 0.7 iota_compare_fusion.1
  8.1 1.0 fusion.20
  9.1 1.3 convolution_bitcast_fusion.1
  10.4 4.7 %convolution_bitcast_fusion = f32[8,8,128]{2,0,1:T(8,128)S(1)} fusion(bf16[4096,1024]{1,0:T(8,128)(2,1)} %param.21, bf16[8,4096]{1,0:T(8,128)(2,1)} %param.19, f32[4096]{0:T(1024)} %param.20, f32[8]{0:T(128)S(1)} %add_rsqrt_fusion.2), kind=kOutput, calls=%fused_computation.18 | convolution fusion | flops 67239936 | bytes 8503328 | tf_op jit(solution)/shard_map/dot_general | solution.py:98
  15.0 0.1 multiply_cosine_fusion
  15.1 0.1 subtract_convert_fusion.1
  15.2 0.1 subtract_convert_fusion
  15.3 0.1 maximum_bitcast_fusion
  15.4 0.2 fusion.34
  15.6 0.0 copy-start.3
  15.6 10.4 %fusion.43 = (f32[8,2,4]{2,1,0:T(2,128)S(1)}, f32[8,2,4,4096]{3,2,1,0:T(4,128)S(1)}) fusion(bf16[8,2,4096,128]{3,2,1,0:T(8,128)(2,1)} %param.25, bf16[8,2,4,64]{3,2,1,0:T(4,128)(2,1)S(1)} %bitcast.51, bf16[8,2,4,64]{3,2,1,0:T(4,128)(2,1)S(1)} %bitcast.49, pred[8,4096]{1,0:T(8,128)(4,1)S(1)} %iota_compare_fusion.1), kind=kOutput, calls=%fused_computation.78 | convolution fusion | flops 67928000 | bytes 17875200 | tf_op jit(solution)/shard_map/rkgd,rkld->rkgl/dot_general | solution.py:55
  26.0 0.5 fusion.13
  26.6 2.0 fusion.12
  28.6 7.1 %fusion.10 = bf16[8,2,4,128]{3,2,1,0:T(4,128)(2,1)S(1)} fusion(bf16[8,2,4096,128]{3,2,1,0:T(8,128)(2,1)} %param.26, f32[8,2,4,4096]{3,2,1,0:T(4,128)S(1)} %get-tuple-element.80, f32[8,2,4]{2,1,0:T(2,128)S(1)} %multiply_maximum_fusion, f32[8,2,4]{2,1,0:T(2,128)S(1)} %get-tuple-element.70, f32[8,2,128]{2,1,0:T(2,128)S(1)} %copy.20, ...), kind=kOutput, calls=%fused_computation.19 | convolution fusion | flops 67665920 | bytes 17851136 | tf_op jit(solution)/shard_map/rkgl,rkld->rkgd/dot_general | solution.py:64
  35.7 0.0 copy-start.4
  35.7 5.2 %convolution_convert_fusion.1 = bf16[8,4096]{1,0:T(8,128)(2,1)} fusion(bf16[8,1024]{1,0:T(8,128)(2,1)S(1)} %reshape.136, bf16[1024,4096]{1,0:T(8,128)(2,1)} %param.24), kind=kOutput, calls=%fused_computation.13 | convolution fusion | flops 67141632 | bytes 8470528 | tf_op jit(solution)/shard_map/dot_general | solution.py:119
  40.9 0.0 all-reduce.7.cloned.1.call-update
  40.9 0.0 reduce-scatter.2.cloned.1.call-start
  41.0 37.3 %all-reduce.7.cloned.1.call-done = bf16[8,4096]{1,0:T(8,128)(2,1)} async-done(((bf16[8,4096]{1,0:T(8,128)(2,1)}), bf16[8,4096]{1,0:T(8,128)(2,1)}) %all-reduce.7.cloned.1.call-update) | async-done | bytes 65552 | tf_op jit(solution)/shard_map/psum | solution.py:124
  78.2 1.0 fusion.24
  79.2 0.1 fusion.26
  79.3 9.8 %all_gather.24 = bf16[64,4096]{1,0:T(8,128)(2,1)S(1)} all-gather(bf16[8,4096]{1,0:T(8,128)(2,1)S(1)} %fusion.26), channel_id=1, replica_groups=mesh['dp'=8,'mp'=4] {'dp'}, dimensions={0}, use_global_device_ids=true | all-gather | bytes 589824 | tf_op jit(solution)/shard_map/all_gather | solution.py:133
  89.2 3.2 %fusion.45 = f32[64,448]{1,0:T(8,128)S(1)} fusion(bf16[64,4096]{1,0:T(8,128)(2,1)S(1)} %all_gather.24, bf16[4096,448]{0,1:T(8,128)(2,1)} %param.30), kind=kOutput, calls=%fused_computation.80 | convolution fusion | flops 234881024 | bytes 4308992 | tf_op jit(solution)/shard_map/dot_general | solution.py:129
  92.4 0.0 copy-start.5
  92.4 6.1 %convolution_convert_fusion = bf16[64,4096]{1,0:T(8,128)(2,1)} fusion(bf16[448,4096]{1,0:T(8,128)(2,1)} %param.32, bf16[64,4096]{1,0:T(8,128)(2,1)S(1)} %all_gather.24, bf16[4096,448]{0,1:T(8,128)(2,1)} %param.31, f32[64,448]{1,0:T(8,128)S(1)} %fusion.45), kind=kOutput, calls=%fused_computation.12 | convolution fusion | flops 470196224 | bytes 8503296 | tf_op jit(solution)/shard_map/dot_general | solution.py:135
  98.5 0.0 reduce-scatter.2.cloned.1.call-update
  98.5 0.0 all-reduce.9.cloned.1.call-start
  98.6 33.1 %reduce-scatter.2.cloned.1.call-done = bf16[8,4096]{1,0:T(8,128)(2,1)} async-done(((bf16[64,4096]{1,0:T(8,128)(2,1)}), bf16[8,4096]{1,0:T(8,128)(2,1)}) %reduce-scatter.2.cloned.1.call-update) | async-done | bytes 65552 | tf_op jit(solution)/shard_map/reduce_scatter | solution.py:134
  131.6 0.0 all-reduce.9.cloned.1.call-update
  131.7 36.7 %all-reduce.9.cloned.1.call-done = bf16[8,4096]{1,0:T(8,128)(2,1)} async-done(((bf16[8,4096]{1,0:T(8,128)(2,1)}), bf16[8,4096]{1,0:T(8,128)(2,1)}) %all-reduce.9.cloned.1.call-update) | async-done | bytes 65552 | tf_op jit(solution)/shard_map/psum | solution.py:144
  168.4 1.0 fusion.17
  169.4 0.9 fusion.19
  170.3 10.0 %all_gather.25 = bf16[64,4096]{1,0:T(8,128)(2,1)S(1)} all-gather(bf16[8,4096]{1,0:T(8,128)(2,1)S(1)} %fusion.19), channel_id=1, replica_groups=mesh['dp'=8,'mp'=4] {'dp'}, dimensions={0}, use_global_device_ids=true | all-gather | bytes 589824 | tf_op jit(solution)/shard_map/all_gather | solution.py:151
  180.3 15.6 %fusion.44 = (f32[64]{0:T(128)S(1)}, f32[64,4008]{1,0:T(8,128)S(1)}) fusion(bf16[64,4096]{1,0:T(8,128)(2,1)S(1)} %all_gather.25, bf16[4096,4008]{0,1:T(8,128)(2,1)} %param.34), kind=kOutput, calls=%fused_computation.79 | convolution fusion | flops 2101602816 | bytes 34384128 | tf_op jit(solution)/shard_map/dot_general | solution.py:149
  195.9 0.5 select_reduce_fusion
  196.4 0.3 dynamic-update-slice
  196.6 0.3 dynamic-update-slice.2
  196.9 0.3 dynamic-update-slice.1
  197.2 39.5 %all-reduce.3 = (f32[2048]{0:T(1024)S(1)}, f32[2048]{0:T(1024)S(1)}, f32[2048]{0:T(1024)S(1)}) all-reduce(f32[2048]{0:T(1024)S(1)} %dynamic-update-slice, f32[2048]{0:T(1024)S(1)} %dynamic-update-slice.1, f32[2048]{0:T(1024)S(1)} %dynamic-update-slice.2), channel_id=2, replica_groups=mesh['dp'=8,'mp'=4] {'dp','mp'}, use_global_device_ids=true, to_apply=%add | all-reduce | flops 6144 | bytes 49152
  236.6 0.1 slice.53
  236.7 0.1 slice.54
  236.8 0.1 slice.55
  236.8 0.1 reshape.147
  236.9 0.1 reshape.148
  237.0 0.1 reshape.149
  237.1 1.4 while.14
  238.5 0.6 compare_select_fusion
  (63 shorter events, 1.1 us)
Async XLA Ops:
  6.5 2.6 %copy-start = (bf16[4096,256]{1,0:T(8,128)(2,1)S(1)}, bf16[4096,256]{1,0:T(8,128)(2,1)}, u32[]{:S(2)}) copy-start(bf16[4096,256]{1,0:T(8,128)(2,1)} %param.22) | copy-start | bytes 6291460
  6.5 71.7 %all-reduce.7.cloned.1.call-start = ((), (), s32[]{:S(2)}) async-start(), calls=%async_computation.1 | async-start | bytes 131072 | tf_op jit(solution)/shard_map/psum | solution.py:124
  15.6 10.9 %copy-start.2 = (bf16[8,4096]{1,0:T(8,128)(2,1)S(1)}, bf16[8,4096]{1,0:T(8,128)(2,1)}, u32[]{:S(2)}) copy-start(bf16[8,4096]{1,0:T(8,128)(2,1)} %param.19) | copy-start | bytes 196612
  15.6 10.9 %copy-start.3 = (f32[4096]{0:T(1024)S(1)}, f32[4096]{0:T(1024)}, u32[]{:S(2)}) copy-start(f32[4096]{0:T(1024)} %param.20) | copy-start | bytes 49156
  35.7 43.5 %copy-start.4 = (f32[4096]{0:T(1024)S(1)}, f32[4096]{0:T(1024)}, u32[]{:S(2)}) copy-start(f32[4096]{0:T(1024)} %param.29) | copy-start | bytes 49156
  40.9 90.7 %reduce-scatter.2.cloned.1.call-start = ((), (), s32[]{:S(2)}) async-start(), calls=%async_computation.2 | async-start | bytes 589824 | tf_op jit(solution)/shard_map/reduce_scatter | solution.py:134
  92.4 39.3 %copy-start.7 = (s32[64]{0:T(128)S(1)}, s32[64]{0:T(128)}, u32[]{:S(2)}) copy-start(s32[64]{0:T(128)} %param.35) | copy-start | bytes 772
  92.4 77.0 %copy-start.5 = (f32[4096]{0:T(1024)S(1)}, f32[4096]{0:T(1024)}, u32[]{:S(2)}) copy-start(f32[4096]{0:T(1024)} %param.33) | copy-start | bytes 49156
  98.5 69.9 %all-reduce.9.cloned.1.call-start = ((), (), s32[]{:S(2)}) async-start(), calls=%async_computation.3 | async-start | bytes 131072 | tf_op jit(solution)/shard_map/psum | solution.py:144
  180.3 58.2 %copy-start.6 = (s32[8]{0:T(128)S(1)}, s32[8]{0:T(128)}, u32[]{:S(2)}) copy-start(s32[8]{0:T(128)} %param.28) | copy-start | bytes 100
  180.3 58.8 %copy-start.1 = (bf16[4096,256]{1,0:T(8,128)(2,1)S(1)}, bf16[4096,256]{1,0:T(8,128)(2,1)}, u32[]{:S(2)}) copy-start(bf16[4096,256]{1,0:T(8,128)(2,1)} %param.22) | copy-start | bytes 6291460
Sparse Core Ops, SparseCore 0:
  41.1 37.1 all-reduce.6
  98.6 32.9 reduce-scatter.1
  133.9 34.3 all-reduce.8
where the time goes:
time: 246 us
  waiting for transfers between devices  107 us (43%)
  blocking collectives  59.3 us (24%)
  matrix products  55.7 us (23%)
  between operations  13.3 us (5%)
  other arithmetic  8.45 us (3%)
    unnamed x1, blocking collectives  39.5 us
    psum x1, waiting for transfers between devices, shards(): lax.psum(partial_heads.astype(jnp.bfloat16), 'mp').astype(jnp.float32)  37.3 us
    psum x1, waiting for transfers between devices, shards(): feed = lax.psum(partial_feed.astype(jnp.bfloat16), 'mp').astype(jnp.float32)  36.7 us
    reduce_scatter x1, waiting for transfers between devices, shards(): lax.psum_scatter(jnp.dot(lax.slice_in_dim(activation, 0, local_rows * lax...  33.1 us
    dot_general x1, matrix products, score_rows(): return jnp.dot(piece, vocab_weight, preferred_element_type=jnp.float32)  15.6 us
    dot_general x1, matrix products, padded_attention(): jnp.einsum('rkgd,rkld->rkgl', queries, key_cache, preferred_element_type=...  10.4 us
    all_gather x1, blocking collectives, shards(): logits = score_rows(lax.all_gather(final, 'dp', axis=0, tiled=True))  10 us
    all_gather x1, blocking collectives, shards(): activation = activate(lax.all_gather(feed_in, 'dp', axis=0, tiled=True))  9.82 us
  transfers between devices with their start and end apart: 3, of which 3 were waited for; matrix products, arithmetic and copies ran while one was open for 0% of the time, Pallas kernels for 0%

commit v1 on v0

--- a/solution.py
+++ b/solution.py
@@ -1,8 +1,11 @@
+import functools
 import math
 
 import jax
 import jax.numpy as jnp
 from jax import lax
+from jax.experimental import pallas as pl
+from jax.experimental.pallas import tpu as pltpu
 from jax.sharding import PartitionSpec as P
 
 H = 32
@@ -12,14 +15,6 @@
 EPSILON = 1e-05
 THETA = 500000.0
 NEGATIVE = -1e30
-
-
-def joined(value, axis, join):
-    pieces = jax.tree.map(lambda part: lax.all_gather(part, axis), value)
-    head = jax.tree.map(lambda part: part[0], pieces)
-    tail = jax.tree.map(lambda part: part[1:], pieces)
-    subtotal, _ = lax.scan(lambda subtotal, piece: (join(subtotal, piece), None), head, tail)
-    return subtotal
 
 
 def rms_norm(hidden, gain):
@@ -42,10 +37,183 @@
     )
 
 
-def combine_parts(former, latter):
-    highest = jnp.maximum(former[0], latter[0])
-    spread = former[1] * jnp.exp(former[0] - highest) + latter[1] * jnp.exp(latter[0] - highest)
-    return (highest, spread, former[2] + latter[2])
+MESH = pl.DeviceIdType.MESH
+VMEM = pltpu.VMEM
+
+
+def greet(n_dp, n_mp):
+    dp, mp = lax.axis_index("dp"), lax.axis_index("mp")
+    barrier = pltpu.get_barrier_semaphore()
+    for step in range(1, n_mp):
+        pl.semaphore_signal(
+            barrier, inc=1, device_id=(dp, lax.rem(mp + step, n_mp)), device_id_type=MESH
+        )
+    for step in range(1, n_dp):
+        pl.semaphore_signal(
+            barrier, inc=1, device_id=(lax.rem(dp + step, n_dp), mp), device_id_type=MESH
+        )
+    pl.semaphore_wait(barrier, n_mp + n_dp - 2)
+    return dp, mp
+
+
+def exchange(sources, targets, sends, receives, peers):
+    copies = []
+    for step, (source, target, peer) in enumerate(zip(sources, targets, peers)):
+        copy = pltpu.make_async_remote_copy(
+            src_ref=source,
+            dst_ref=target,
+            send_sem=sends.at[step],
+            recv_sem=receives.at[step],
+            device_id=peer,
+            device_id_type=MESH,
+        )
+        copy.start()
+        copies.append(copy)
+    return copies
+
+
+def across_mp(dp, mp, n_mp):
+    return [(dp, lax.rem(mp + step, n_mp)) for step in range(1, n_mp)]
+
+
+def across_dp(dp, mp, n_dp):
+    return [(lax.rem(dp + step, n_dp), mp) for step in range(1, n_dp)]
+
+
+def normalized(wide, gain):
+    scale = lax.rsqrt(jnp.mean(wide * wide, axis=-1, keepdims=True) + EPSILON)
+    return (wide * scale * gain).astype(jnp.bfloat16)
+
+
+def spread_rows(gathered_ref, dp, mp, n_dp, sends, receives):
+    mine = gathered_ref.at[dp]
+    copies = exchange(
+        [mine] * (n_dp - 1),
+        [mine] * (n_dp - 1),
+        sends,
+        receives,
+        across_dp(dp, mp, n_dp),
+    )
+    for copy in copies:
+        copy.wait()
+
+
+def after_attention(
+    n_dp, n_mp, partial_ref, hidden_ref, gain_ref, gathered_ref, mixed_ref,
+    landed, mp_send, mp_receive, dp_send, dp_receive,
+):
+    dp, mp = greet(n_dp, n_mp)
+    copies = exchange(
+        [partial_ref] * (n_mp - 1),
+        [landed.at[step] for step in range(n_mp - 1)],
+        mp_send,
+        mp_receive,
+        across_mp(dp, mp, n_mp),
+    )
+    total = partial_ref[...].astype(jnp.float32)
+    for step, copy in enumerate(copies):
+        copy.wait()
+        total = total + landed[step].astype(jnp.float32)
+    mixed = (hidden_ref[...].astype(jnp.float32) + total).astype(jnp.bfloat16)
+    mixed_ref[...] = mixed
+    gathered_ref[dp] = normalized(mixed.astype(jnp.float32), gain_ref[...])
+    spread_rows(gathered_ref, dp, mp, n_dp, dp_send, dp_receive)
+
+
+def after_feed(
+    n_dp, n_mp, partial_ref, mixed_ref, gain_ref, gathered_ref,
+    arrived, summed, landed, rs_send, rs_receive, mp_send, mp_receive, dp_send, dp_receive,
+):
+    dp, mp = greet(n_dp, n_mp)
+    copies = exchange(
+        [partial_ref.at[lax.rem(dp + step, n_dp)] for step in range(1, n_dp)],
+        [arrived.at[step] for step in range(n_dp - 1)],
+        rs_send,
+        rs_receive,
+        across_dp(dp, mp, n_dp),
+    )
+    total = partial_ref[dp].astype(jnp.float32)
+    for step, copy in enumerate(copies):
+        copy.wait()
+        total = total + arrived[step].astype(jnp.float32)
+    summed[...] = total.astype(jnp.bfloat16)
+    copies = exchange(
+        [summed] * (n_mp - 1),
+        [landed.at[step] for step in range(n_mp - 1)],
+        mp_send,
+        mp_receive,
+        across_mp(dp, mp, n_mp),
+    )
+    total = summed[...].astype(jnp.float32)
+    for step, copy in enumerate(copies):
+        copy.wait()
+        total = total + landed[step].astype(jnp.float32)
+    residual = (mixed_ref[...].astype(jnp.float32) + total).astype(jnp.bfloat16)
+    gathered_ref[dp] = normalized(residual.astype(jnp.float32), gain_ref[...])
+    spread_rows(gathered_ref, dp, mp, n_dp, dp_send, dp_receive)
+
+
+def joined_stats(pieces):
+    highest = pieces[0][0:1]
+    for piece in pieces[1:]:
+        highest = jnp.maximum(highest, piece[0:1])
+    spread = sum(piece[1:2] * jnp.exp(piece[0:1] - highest) for piece in pieces)
+    picked = sum(piece[2:3] for piece in pieces)
+    return highest, spread, picked
+
+
+def after_logits(
+    n_dp, n_mp, stats_ref, out_ref,
+    landed, joint, arrived, mp_send, mp_receive, dp_send, dp_receive,
+):
+    dp, mp = greet(n_dp, n_mp)
+    copies = exchange(
+        [stats_ref] * (n_mp - 1),
+        [landed.at[step] for step in range(n_mp - 1)],
+        mp_send,
+        mp_receive,
+        across_mp(dp, mp, n_mp),
+    )
+    for copy in copies:
+        copy.wait()
+    highest, spread, picked = joined_stats(
+        [stats_ref[...]] + [landed[step] for step in range(n_mp - 1)]
+    )
+    joint[...] = jnp.zeros_like(joint)
+    joint[0:1] = highest
+    joint[1:2] = spread
+    joint[2:3] = picked
+    copies = exchange(
+        [joint] * (n_dp - 1),
+        [arrived.at[step] for step in range(n_dp - 1)],
+        dp_send,
+        dp_receive,
+        across_dp(dp, mp, n_dp),
+    )
+    for copy in copies:
+        copy.wait()
+    highest, spread, picked = joined_stats(
+        [joint[...]] + [arrived[step] for step in range(n_dp - 1)]
+    )
+    result = picked - (highest + jnp.log(spread))
+    out_ref[...] = jnp.broadcast_to(result, out_ref.shape)
+
+
+def pairs(count):
+    return [pltpu.SemaphoreType.DMA((max(count, 1),))] * 2
+
+
+def comm_call(kernel, operands, out_shape, scratch, number):
+    return pl.pallas_call(
+        kernel,
+        out_shape=out_shape,
+        in_specs=[pl.BlockSpec(memory_space=VMEM)] * len(operands),
+        out_specs=jax.tree.map(lambda _: pl.BlockSpec(memory_space=VMEM), out_shape),
+        scratch_shapes=scratch,
+        compiler_params=pltpu.CompilerParams(
+            collective_id=number, has_side_effects=True, vmem_limit_bytes=8 * 1024 * 1024
+        ),
+    )(*operands)
 
 
 def padded_attention(queries, own, key_cache, value_cache, new_values, lengths):
@@ -121,45 +289,69 @@
         output_weight,
         preferred_element_type=jnp.float32,
     )
-    attention = lax.psum(partial_heads.astype(jnp.bfloat16), "mp").astype(jnp.float32)
-    mixed_hidden = (hidden.astype(jnp.float32) + attention).astype(jnp.bfloat16)
-    feed_in = rms_norm(mixed_hidden, feed_gain)
-
-    def activate(piece):
-        gate = jnp.dot(piece, gate_weight, preferred_element_type=jnp.float32)
-        upward = jnp.dot(piece, up_weight, preferred_element_type=jnp.float32)
-        return (jax.nn.silu(gate) * upward).astype(jnp.bfloat16)
-
-    activation = activate(lax.all_gather(feed_in, "dp", axis=0, tiled=True))
-    partial_feed = lax.psum_scatter(
-        jnp.dot(
-            lax.slice_in_dim(activation, 0, local_rows * lax.axis_size("dp"), axis=0),
-            down_weight,
-            preferred_element_type=jnp.float32,
-        ).astype(jnp.bfloat16),
-        "dp",
-        scatter_dimension=0,
-        tiled=True,
-    ).astype(jnp.float32)
-    feed = lax.psum(partial_feed.astype(jnp.bfloat16), "mp").astype(jnp.float32)
-    residual = (mixed_hidden.astype(jnp.float32) + feed).astype(jnp.bfloat16)
-    final = rms_norm(residual, final_gain)
-
-    def score_rows(piece):
-        return jnp.dot(piece, vocab_weight, preferred_element_type=jnp.float32)
-
-    logits = score_rows(lax.all_gather(final, "dp", axis=0, tiled=True))
+    n_dp, n_mp = lax.axis_size("dp"), lax.axis_size("mp")
+    width = hidden.shape[1]
+    row_type = jax.ShapeDtypeStruct((local_rows, width), jnp.bfloat16)
+    all_rows = jax.ShapeDtypeStruct((n_dp, local_rows, width), jnp.bfloat16)
+    landing = VMEM((max(n_mp - 1, 1), local_rows, width), jnp.bfloat16)
+    feed_in, mixed_hidden = comm_call(
+        functools.partial(after_attention, n_dp, n_mp),
+        (partial_heads.astype(jnp.bfloat16), hidden, feed_gain[None]),
+        (all_rows, row_type),
+        [landing] + pairs(n_mp - 1) + pairs(n_dp - 1),
+        1,
+    )
+    feed_in = feed_in.reshape(n_dp * local_rows, width)
+    gate = jnp.dot(feed_in, gate_weight, preferred_element_type=jnp.float32)
+    upward = jnp.dot(feed_in, up_weight, preferred_element_type=jnp.float32)
+    activation = (jax.nn.silu(gate) * upward).astype(jnp.bfloat16)
+    partial_feed = jnp.dot(activation, down_weight, preferred_element_type=jnp.float32)
+    final = comm_call(
+        functools.partial(after_feed, n_dp, n_mp),
+        (
+            partial_feed.astype(jnp.bfloat16).reshape(n_dp, local_rows, width),
+            mixed_hidden,
+            final_gain[None],
+        ),
+        all_rows,
+        [
+            VMEM((n_dp - 1, local_rows, width), jnp.bfloat16),
+            VMEM((local_rows, width), jnp.bfloat16),
+            landing,
+        ]
+        + pairs(n_dp - 1)
+        + pairs(n_mp - 1)
+        + pairs(n_dp - 1),
+        2,
+    )
+    final = final.reshape(n_dp * local_rows, width)
+    logits = jnp.dot(final, vocab_weight, preferred_element_type=jnp.float32)
     vocab_local = vocab_weight.shape[1]
-    vocab_start = (lax.axis_index("dp") * lax.axis_size("mp") + lax.axis_index("mp")) * vocab_local
+    vocab_start = (lax.axis_index("dp") * n_mp + lax.axis_index("mp")) * vocab_local
     offsets = next_tokens - vocab_start
     matches = lax.broadcasted_iota(jnp.int32, (1, vocab_local), 1) == offsets[:, None]
     picked = jnp.sum(jnp.where(matches, logits, 0.0), axis=-1)
     local_top = jnp.max(logits, axis=-1)
     local_spread = jnp.sum(jnp.exp(logits - local_top[:, None]), axis=-1)
-    top, spread_sum, picked = joined((local_top, local_spread, picked), ("dp", "mp"), combine_parts)
-    normalizer = top + jnp.log(spread_sum)
-    row_start = lax.axis_index("dp") * local_rows
-    chosen = lax.dynamic_slice_in_dim(picked - normalizer, row_start, local_rows, 0)
+    rollouts = next_tokens.shape[0]
+    lanes = -(-rollouts // 128) * 128
+    stats = jnp.pad(
+        jnp.stack([local_top, local_spread, picked]), ((0, 5), (0, lanes - rollouts))
+    )
+    chosen = comm_call(
+        functools.partial(after_logits, n_dp, n_mp),
+        (stats,),
+        jax.ShapeDtypeStruct((8, lanes), jnp.float32),
+        [
+            VMEM((max(n_mp - 1, 1), 8, lanes), jnp.float32),
+            VMEM((8, lanes), jnp.float32),
+            VMEM((n_dp - 1, 8, lanes), jnp.float32),
+        ]
+        + pairs(n_mp - 1)
+        + pairs(n_dp - 1),
+        3,
+    )
+    chosen = lax.dynamic_slice_in_dim(chosen[0], lax.axis_index("dp") * local_rows, local_rows, 0)
     return jnp.where(finished != 0, 0.0, chosen).astype(jnp.float32)
 
 

time: 246 us -> 110 us (0.45)
  waiting for transfers between devices: 107 us -> 0 us
  blocking collectives: 59.3 us -> 0 us
  Pallas kernels: 0 us -> 52.8 us
  between operations: 13.3 us -> 0.26 us
  other arithmetic: 8.45 us -> 3.86 us
  matrix products: 55.7 us -> 52.6 us
    psum x2 -> x0, waiting for transfers between devices: 74 us -> none  [the longest x1 37.3 us: shards(): lax.psum(partial_heads.astype(jnp.bfloat16), 'mp').astype(jnp.float32)]
    pallas_call x0 -> x3, Pallas kernels: none -> 52.8 us  [comm_call(): pl.pallas_call(kernel, out_shape=out_shape, in_specs=[pl.BlockSpec(memory...]
    unnamed x1 -> x0, blocking collectives: 39.5 us -> none
    reduce_scatter x1 -> x0, waiting for transfers between devices: 33.1 us -> none  [shards(): lax.psum_scatter(jnp.dot(lax.slice_in_dim(activation, 0, local_rows * lax...]
    all_gather x2 -> x0, blocking collectives: 19.8 us -> none  [the longest x1 10 us: shards(): logits = score_rows(lax.all_gather(final, 'dp', axis=0, tiled=True))]
    dot_general x3, matrix products: 24.9 us -> 22.1 us  [the longest x1 15.6 us: shards(): logits = jnp.dot(final, vocab_weight, preferred_element_type=jnp.float32)]
  transfers between devices with their start and end apart: 3 -> 0, of which waited for: 3 -> 0; matrix products, arithmetic and copies ran while one was open for 0% -> 0% of each run, Pallas kernels for 0% -> 0%
where the time goes in v1:
time: 110 us
  Pallas kernels  52.8 us (48%)
  matrix products  52.6 us (48%)
  other arithmetic  3.86 us (4%)
    pallas_call x3, Pallas kernels, comm_call(): pl.pallas_call(kernel, out_shape=out_shape, in_specs=[pl.BlockSpec(memory...  52.8 us
    dot_general x1, matrix products, shards(): logits = jnp.dot(final, vocab_weight, preferred_element_type=jnp.float32)  15.6 us
    dot_general x1, matrix products, padded_attention(): jnp.einsum('rkgd,rkld->rkgl', queries, key_cache, preferred_element_type=...  10.4 us
    dot_general x1, matrix products, padded_attention(): jnp.einsum('rkgl,rkld->rkgd', weights.astype(jnp.bfloat16), value_cache,...  7.27 us
    dot_general x1, matrix products, shards(): jnp.dot(activation, down_weight, preferred_element_type=jnp.float32)  5.29 us
    dot_general x1, matrix products, shards(): jnp.dot(attended.reshape(local_rows, key_heads * groups * head_width), ou...  4.72 us
    dot_general x1, matrix products, shards(): jnp.dot(normed, query_weight, preferred_element_type=jnp.float32)  4.68 us

profile of v1, /device:TPU:0, one launch (start us, length us, event | category | flops | bytes accessed | tf_op | source)
XLA Modules:
  0.0 109.6 jit_solution(11366852884928657360)
XLA Ops:
  0.0 0.0 copy-start
  0.0 0.8 convert_element_type.45
  0.8 0.1 multiply_cosine_fusion
  0.9 1.0 fusion.17
  1.9 0.0 copy-done
  1.9 1.3 %convolution_bitcast_fusion.1 = f32[8,2,128]{2,0,1:T(8,128)S(1)} fusion(bf16[4096,256]{1,0:T(8,128)(2,1)S(1)} %copy-done, bf16[8,4096]{1,0:T(8,128)(2,1)} %hidden_ref.1, f32[4096]{0:T(1024)} %param.18, f32[8]{0:T(128)S(1)} %add_rsqrt_fusion), kind=kOutput, calls=%fused_computation.11 | convolution fusion | flops 16908288 | bytes 2187296 | tf_op jit(solution)/shard_map/dot_general | solution.py:274
  3.2 0.1 subtract_convert_fusion.1
  3.3 0.1 maximum_bitcast_fusion
  3.4 0.0 copy-start.7
  3.4 4.7 %convolution_bitcast_fusion = f32[8,8,128]{2,0,1:T(8,128)S(1)} fusion(bf16[4096,1024]{1,0:T(8,128)(2,1)} %param.19, bf16[8,4096]{1,0:T(8,128)(2,1)} %hidden_ref.1, f32[4096]{0:T(1024)} %param.18, f32[8]{0:T(128)S(1)} %add_rsqrt_fusion), kind=kOutput, calls=%fused_computation.9 | convolution fusion | flops 67239936 | bytes 8503328 | tf_op jit(solution)/shard_map/dot_general | solution.py:266
  8.0 0.1 subtract_convert_fusion
  8.2 0.2 fusion.26
  8.4 0.0 copy-done.7
  8.4 0.1 iota_compare_fusion.1
  8.5 0.0 copy-start.2
  8.5 0.0 copy-start.6
  8.5 10.4 %fusion.33 = (f32[8,2,4]{2,1,0:T(2,128)S(1)}, f32[8,2,4,4096]{3,2,1,0:T(4,128)S(1)}) fusion(bf16[8,2,4096,128]{3,2,1,0:T(8,128)(2,1)} %param.23, bf16[8,2,4,64]{3,2,1,0:T(4,128)(2,1)S(1)} %bitcast.51, bf16[8,2,4,64]{3,2,1,0:T(4,128)(2,1)S(1)} %bitcast.49, pred[8,4096]{1,0:T(8,128)(4,1)S(1)} %iota_compare_fusion.1), kind=kOutput, calls=%fused_computation.61 | convolution fusion | flops 67928000 | bytes 17875200 | tf_op jit(solution)/shard_map/rkgd,rkld->rkgl/dot_general | solution.py:223
  18.9 0.5 fusion.7
  19.4 0.0 copy-done.2
  19.4 0.0 copy-done.6
  19.4 2.0 %fusion.6 = f32[8,2,128]{2,0,1:T(8,128)S(1)} fusion(bf16[4096,256]{1,0:T(8,128)(2,1)} %param.21, bf16[8,4096]{1,0:T(8,128)(2,1)S(1)} %copy-done.2, f32[4096]{0:T(1024)S(1)} %copy-done.6, f32[8]{0:T(128)S(1)} %add_rsqrt_fusion), kind=kOutput, calls=%fused_computation.14 | convolution fusion | flops 16912384 | bytes 2187296 | tf_op jit(solution)/shard_map/dot_general | solution.py:279
  21.4 7.3 %fusion.4 = bf16[8,2,4,128]{3,2,1,0:T(4,128)(2,1)S(1)} fusion(bf16[8,2,4096,128]{3,2,1,0:T(8,128)(2,1)} %param.24, f32[8,2,4,4096]{3,2,1,0:T(4,128)S(1)} %get-tuple-element.20, f32[8,2,4]{2,1,0:T(2,128)S(1)} %multiply_maximum_fusion, f32[8,2,4]{2,1,0:T(2,128)S(1)} %get-tuple-element.11, f32[8,2,128]{2,1,0:T(2,128)S(1)} %copy.20, ...), kind=kOutput, calls=%fused_computation.10 | convolution fusion | flops 67665920 | bytes 17851136 | tf_op jit(solution)/shard_map/rkgl,rkld->rkgd/dot_general | solution.py:232
  28.7 0.0 copy-start.4
  28.8 0.0 copy-start.5
  28.8 4.7 %convolution_convert_fusion.1.partial_ref = bf16[8,4096]{1,0:T(8,128)(2,1)S(1)} fusion(bf16[8,1024]{1,0:T(8,128)(2,1)S(1)} %reshape.128, bf16[1024,4096]{1,0:T(8,128)(2,1)} %param.22), kind=kOutput, calls=%fused_computation.4 | convolution fusion | flops 67141632 | bytes 8470528 | tf_op jit(solution)/shard_map/dot_general | solution.py:287
  33.5 0.0 copy-done.4
  33.5 17.2 %shard_map.163 = (bf16[8,8,4096]{2,1,0:T(8,128)(2,1)S(1)}, bf16[8,4096]{1,0:T(8,128)(2,1)S(1)}) custom-call(bf16[8,4096]{1,0:T(8,128)(2,1)S(1)} %convolution_convert_fusion.1.partial_ref, bf16[8,4096]{1,0:T(8,128)(2,1)S(1)} %copy-done.2, f32[1,4096]{1,0:T(1,128)S(1)} %bitcast.47), custom_call_target="tpu_custom_call" | custom-call | tf_op jit(solution)/shard_map/pallas_call | solution.py:207
  50.7 0.0 copy-done.5
  50.7 1.2 %fusion.14 = f32[64,448]{1,0:T(8,128)S(1)} fusion(bf16[4096,448]{0,1:T(8,128)(2,1)S(1)} %copy-done.5, bf16[8,8,4096]{2,1,0:T(8,128)(2,1)S(1)} %get-tuple-element.7), kind=kOutput, calls=%fused_computation.24 | convolution fusion | flops 234881024 | bytes 4308992 | tf_op jit(solution)/shard_map/dot_general | solution.py:305
  51.8 0.0 copy-start.3
  51.9 5.3 %fusion.1.partial_ref = bf16[8,8,4096]{2,1,0:T(8,128)(2,1)S(1)} fusion(bf16[448,4096]{1,0:T(8,128)(2,1)} %param.30, bf16[4096,448]{0,1:T(8,128)(2,1)} %param.29, bf16[8,8,4096]{2,1,0:T(8,128)(2,1)S(1)} %get-tuple-element.7, f32[64,448]{1,0:T(8,128)S(1)} %fusion.14), kind=kOutput, calls=%fused_computation.3 | convolution fusion | flops 470196224 | bytes 8503296 | tf_op jit(solution)/shard_map/dot_general | solution.py:308
  57.2 0.0 copy-done.3
  57.2 24.4 %shard_map.164 = bf16[8,8,4096]{2,1,0:T(8,128)(2,1)S(1)} custom-call(bf16[8,8,4096]{2,1,0:T(8,128)(2,1)S(1)} %fusion.1.partial_ref, bf16[8,4096]{1,0:T(8,128)(2,1)S(1)} %get-tuple-element.8.mixed_ref, f32[1,4096]{1,0:T(1,128)S(1)} %bitcast.46), custom_call_target="tpu_custom_call" | custom-call | tf_op jit(solution)/shard_map/pallas_call | solution.py:207
  81.6 0.0 copy-start.9
  81.6 0.0 copy-start.8
  81.6 0.0 copy-start.1
  81.7 15.6 %fusion.34 = (f32[64]{0:T(128)S(1)}, f32[64,4008]{1,0:T(8,128)S(1)}) fusion(bf16[4096,4008]{0,1:T(8,128)(2,1)} %param.32, bf16[8,8,4096]{2,1,0:T(8,128)(2,1)S(1)} %shard_map.164), kind=kOutput, calls=%fused_computation.62 | convolution fusion | flops 2101602816 | bytes 34384128 | tf_op jit(solution)/shard_map/dot_general | solution.py:328
  97.3 0.0 copy-done.9
  97.3 0.5 exponential_reduce_fusion
  97.8 11.2 %shard_map.165 = f32[8,128]{1,0:T(8,128)S(1)} custom-call(f32[8,128]{1,0:T(8,128)S(1)} %select_maximum_fusion.stats_ref), custom_call_target="tpu_custom_call" | custom-call | tf_op jit(solution)/shard_map/pallas_call | solution.py:207
  109.0 0.0 copy-done.8
  109.0 0.6 compare_select_fusion
  109.6 0.0 copy-done.1
  (11 shorter events, 0.1 us)
Async XLA Ops:
  0.0 1.9 %copy-start = (bf16[4096,256]{1,0:T(8,128)(2,1)S(1)}, bf16[4096,256]{1,0:T(8,128)(2,1)}, u32[]{:S(2)}) copy-start(bf16[4096,256]{1,0:T(8,128)(2,1)} %param.20) | copy-start | bytes 6291460
  3.4 5.0 %copy-start.7 = (s32[8]{0:T(128)S(1)}, s32[8]{0:T(128)}, u32[]{:S(2)}) copy-start(s32[8]{0:T(128)} %param.25) | copy-start | bytes 100
  8.5 10.9 %copy-start.2 = (bf16[8,4096]{1,0:T(8,128)(2,1)S(1)}, bf16[8,4096]{1,0:T(8,128)(2,1)}, u32[]{:S(2)}) copy-start(bf16[8,4096]{1,0:T(8,128)(2,1)} %hidden_ref.1) | copy-start | bytes 196612
  8.5 10.9 %copy-start.6 = (f32[4096]{0:T(1024)S(1)}, f32[4096]{0:T(1024)}, u32[]{:S(2)}) copy-start(f32[4096]{0:T(1024)} %param.18) | copy-start | bytes 49156
  28.7 4.8 %copy-start.4 = (f32[4096]{0:T(1024)S(1)}, f32[4096]{0:T(1024)}, u32[]{:S(2)}) copy-start(f32[4096]{0:T(1024)} %param.27) | copy-start | bytes 49156
  28.8 21.9 %copy-start.5 = (bf16[4096,448]{0,1:T(8,128)(2,1)S(1)}, bf16[4096,448]{0,1:T(8,128)(2,1)}, u32[]{:S(2)}) copy-start(bf16[4096,448]{0,1:T(8,128)(2,1)} %param.28) | copy-start | bytes 11010052
  51.8 5.3 %copy-start.3 = (f32[4096]{0:T(1024)S(1)}, f32[4096]{0:T(1024)}, u32[]{:S(2)}) copy-start(f32[4096]{0:T(1024)} %param.31) | copy-start | bytes 49156
  81.6 15.6 %copy-start.9 = (s32[64]{0:T(128)S(1)}, s32[64]{0:T(128)}, u32[]{:S(2)}) copy-start(s32[64]{0:T(128)} %param.33) | copy-start | bytes 772
  81.6 27.4 %copy-start.8 = (s32[8]{0:T(128)S(1)}, s32[8]{0:T(128)}, u32[]{:S(2)}) copy-start(s32[8]{0:T(128)} %param.26) | copy-start | bytes 100
  81.6 28.0 %copy-start.1 = (bf16[4096,256]{1,0:T(8,128)(2,1)S(1)}, bf16[4096,256]{1,0:T(8,128)(2,1)}, u32[]{:S(2)}) copy-start(bf16[4096,256]{1,0:T(8,128)(2,1)} %param.20) | copy-start | bytes 6291460

commit v2 on v1

--- a/solution.py
+++ b/solution.py
@@ -87,15 +87,38 @@
 
 def spread_rows(gathered_ref, dp, mp, n_dp, sends, receives):
     mine = gathered_ref.at[dp]
-    copies = exchange(
-        [mine] * (n_dp - 1),
-        [mine] * (n_dp - 1),
-        sends,
-        receives,
-        across_dp(dp, mp, n_dp),
-    )
-    for copy in copies:
-        copy.wait()
+    if n_dp % 2 == 1 or n_dp == 2:
+        copies = exchange(
+            [mine] * (n_dp - 1),
+            [mine] * (n_dp - 1),
+            sends,
+            receives,
+            across_dp(dp, mp, n_dp),
+        )
+        for copy in copies:
+            copy.wait()
+        return
+    half = n_dp // 2
+    twin = (dp + 1 - 2 * lax.rem(dp, 2), mp)
+    peers = [(lax.rem(dp + 2 * step, n_dp), mp) for step in range(1, half)]
+    copies = exchange([mine] * half, [mine] * half, sends, receives, peers + [twin])
+    for step in range(1, half):
+        copies[step - 1].wait_recv()
+        rows = gathered_ref.at[lax.rem(dp - 2 * step + n_dp, n_dp)]
+        forward = pltpu.make_async_remote_copy(
+            src_ref=rows,
+            dst_ref=rows,
+            send_sem=sends.at[half - 1 + step],
+            recv_sem=receives.at[half - 1 + step],
+            device_id=twin,
+            device_id_type=MESH,
+        )
+        forward.start()
+        copies.append(forward)
+    for place, copy in enumerate(copies):
+        copy.wait_send()
+        if place >= half - 1:
+            copy.wait_recv()
 
 
 def after_attention(
@@ -216,27 +239,142 @@
     )(*operands)
 
 
-def padded_attention(queries, own, key_cache, value_cache, new_values, lengths):
-    head_width = queries.shape[-1]
-    scale = 1.0 / math.sqrt(head_width)
-    scores = (
-        jnp.einsum("rkgd,rkld->rkgl", queries, key_cache, preferred_element_type=jnp.float32)
-        * scale
-    )
-    places = lax.broadcasted_iota(jnp.int32, (1, 1, 1, key_cache.shape[2]), 3)
-    scores = jnp.where(places < lengths[:, None, None, None], scores, NEGATIVE)
-    top = jnp.maximum(jnp.max(scores, axis=-1), own)
-    weights = jnp.exp(scores - top[..., None])
-    own_weight = jnp.exp(own - top)
-    total = jnp.sum(weights, axis=-1) + own_weight
-    mixed = jnp.einsum(
-        "rkgl,rkld->rkgd",
-        weights.astype(jnp.bfloat16),
+def ragged_attention(
+    block, lengths_ref, query_ref, key_ref, value_ref, key_hbm, value_hbm, out_ref,
+    keys, values, key_sem, value_sem, tops, totals, sums,
+):
+    rollouts, heads, width = query_ref.shape
+    key_heads = key_ref.shape[1]
+    groups = heads // key_heads
+    depth = keys.shape[0]
+    scale = 1.0 / math.sqrt(width)
+    owner = lax.broadcasted_iota(jnp.int32, (heads, 1), 0) // groups
+
+    def by_head(pieces):
+        joint = pieces[0]
+        for head in range(1, key_heads):
+            joint = jnp.where(owner == head, pieces[head], joint)
+        return joint
+
+    def blocks_of(row):
+        return lax.div(lengths_ref[jnp.minimum(row, rollouts - 1)] + (block - 1), block)
+
+    def following(row, part):
+        last = part + 1 >= blocks_of(row)
+        return jnp.where(last, row + 1, row), jnp.where(last, 0, part + 1)
+
+    def copies(slot, row, part):
+        places = pl.ds(pl.multiple_of(part * block, block), block)
+        return (
+            pltpu.make_async_copy(
+                key_hbm.at[row, :, places, :], keys.at[slot], key_sem.at[slot]
+            ),
+            pltpu.make_async_copy(
+                value_hbm.at[row, :, places, :], values.at[slot], value_sem.at[slot]
+            ),
+        )
+
+    def fetch(slot, row, part):
+        for copy in copies(slot, row, part):
+            copy.start()
+
+    steps = sum(blocks_of(row) for row in range(rollouts))
+    ahead = (jnp.int32(0), jnp.int32(0))
+    for slot in range(depth - 1):
+        def begin(slot=slot, ahead=ahead):
+            fetch(slot, *ahead)
+
+        pl.when(slot < steps)(begin)
+        ahead = following(*ahead)
+
+    def step_body(step, carry):
+        row, part, ahead_row, ahead_part = carry
+        slot = lax.rem(step, depth)
+
+        @pl.when(step + (depth - 1) < steps)
+        def _():
+            fetch(lax.rem(step + (depth - 1), depth), ahead_row, ahead_part)
+
+        query = query_ref[row]
+
+        @pl.when(part == 0)
+        def _():
+            own_key = by_head([key_ref[row, head : head + 1] for head in range(key_heads)])
+            own_value = by_head([value_ref[row, head : head + 1] for head in range(key_heads)])
+            own = jnp.sum(query * own_key, axis=-1, keepdims=True) * scale
+            tops[...] = jnp.broadcast_to(own, tops.shape)
+            totals[...] = jnp.ones_like(totals)
+            sums[...] = jnp.broadcast_to(own_value, sums.shape)
+
+        key_copy, value_copy = copies(slot, row, part)
+        key_copy.wait()
+        narrow = query.astype(jnp.bfloat16)
+        scores = by_head(
+            [
+                lax.dot_general(
+                    narrow,
+                    keys[slot, head],
+                    (((1,), (1,)), ((), ())),
+                    preferred_element_type=jnp.float32,
+                )
+                for head in range(key_heads)
+            ]
+        )
+        places = part * block + lax.broadcasted_iota(jnp.int32, (1, block), 1)
+        scores = jnp.where(places < lengths_ref[row], scores * scale, NEGATIVE)
+        former = tops[:, 0:1]
+        top = jnp.maximum(former, jnp.max(scores, axis=-1, keepdims=True))
+        fade = jnp.exp(former - top)
+        weights = jnp.exp(scores - top)
+        total = totals[:, 0:1] * fade + jnp.sum(weights, axis=-1, keepdims=True)
+        rounded = weights.astype(jnp.bfloat16)
+        value_copy.wait()
+        mixed = by_head(
+            [
+                jnp.dot(rounded, values[slot, head], preferred_element_type=jnp.float32)
+                for head in range(key_heads)
+            ]
+        )
+        mixed = sums[...] * fade + mixed
+        tops[...] = jnp.broadcast_to(top, tops.shape)
+        totals[...] = jnp.broadcast_to(total, totals.shape)
+        sums[...] = mixed
+        out_ref[row] = (mixed / total).astype(jnp.bfloat16)
+        return following(row, part) + following(ahead_row, ahead_part)
+
+    lax.fori_loop(0, steps, step_body, (jnp.int32(0), jnp.int32(0)) + ahead)
+
+
+def cached_attention(queries, new_keys, new_values, key_cache, value_cache, lengths):
+    rollouts, key_heads, places, width = key_cache.shape
+    heads = queries.shape[1]
+    block = math.gcd(places, 2048)
+    buffers = VMEM((3, key_heads, block, width), jnp.bfloat16)
+    whole = pl.BlockSpec(memory_space=VMEM)
+    away = pl.BlockSpec(memory_space=pl.ANY)
+    return pl.pallas_call(
+        functools.partial(ragged_attention, block),
+        out_shape=jax.ShapeDtypeStruct((rollouts, heads, width), jnp.bfloat16),
+        in_specs=[pl.BlockSpec(memory_space=pltpu.SMEM), whole, whole, whole, away, away],
+        out_specs=whole,
+        scratch_shapes=[
+            buffers,
+            buffers,
+            pltpu.SemaphoreType.DMA((3,)),
+            pltpu.SemaphoreType.DMA((3,)),
+            VMEM((heads, 128), jnp.float32),
+            VMEM((heads, 128), jnp.float32),
+            VMEM((heads, width), jnp.float32),
+        ],
+        compiler_params=pltpu.CompilerParams(vmem_limit_bytes=24 * 1024 * 1024),
+    )(
+        lengths,
+        queries.astype(jnp.float32),
+        new_keys.astype(jnp.float32),
+        new_values.astype(jnp.float32),
+        key_cache,
         value_cache,
-        preferred_element_type=jnp.float32,
-    )
-    mixed = mixed + own_weight[..., None] * new_values.astype(jnp.float32)[:, :, None, :]
-    return (mixed / total[..., None]).astype(jnp.bfloat16)
+    )
 
 
 def shards(
@@ -266,11 +404,7 @@
     queries = jnp.dot(normed, query_weight, preferred_element_type=jnp.float32).reshape(
         local_rows, key_heads * groups, head_width
     )
-    queries = (
-        rotate(queries, lengths)
-        .astype(jnp.bfloat16)
-        .reshape(local_rows, key_heads, groups, head_width)
-    )
+    queries = rotate(queries, lengths).astype(jnp.bfloat16)
     new_keys = jnp.dot(normed, key_weight, preferred_element_type=jnp.float32).reshape(
         local_rows, key_heads, head_width
     )
@@ -280,10 +414,9 @@
         .astype(jnp.bfloat16)
         .reshape(local_rows, key_heads, head_width)
     )
-    own = jnp.einsum("rkgd,rkd->rkg", queries, new_keys, preferred_element_type=jnp.float32) * (
-        1.0 / math.sqrt(head_width)
-    )
-    attended = padded_attention(queries, own, key_cache, value_cache, new_values, lengths)
+    attended = cached_attention(
+        queries, new_keys, new_values, key_cache, value_cache, lengths
+    )
     partial_heads = jnp.dot(
         attended.reshape(local_rows, key_heads * groups * head_width),
         output_weight,

time: 110 us -> 104 us (0.945)
  matrix products: 52.6 us -> 30.4 us
  Pallas kernels: 52.8 us -> 64.9 us
  local copies, waits for them, and re-layouts: 0.09 us -> 5.87 us
  other arithmetic: 3.86 us -> 2.66 us
    dot_general x3 -> x0, matrix products: 17.8 us -> none  [the longest x1 10.4 us: padded_attention(): jnp.einsum('rkgd,rkld->rkgl', queries, key_cache, preferred_element_type=...]
    pallas_call x0 -> x1, Pallas kernels: none -> 15.4 us  [cached_attention(): pl.pallas_call(functools.partial(ragged_attention, block), out_shape=jax....]
    unnamed x20 -> x25, local copies, waits for them, and re-layouts: 0.06 us -> 5.84 us
    dot_general x1, matrix products: 4.72 us -> 1.19 us  [shards(): jnp.dot(attended.reshape(local_rows, key_heads * groups * head_width), ou...]
    pallas_call x3, Pallas kernels: 52.8 us -> 49.5 us  [comm_call(): pl.pallas_call(kernel, out_shape=out_shape, in_specs=[pl.BlockSpec(memory...]
where the time goes in v2:
time: 104 us
  Pallas kernels  64.9 us (62%)
  matrix products  30.4 us (29%)
  local copies, waits for them, and re-layouts  5.87 us (6%)
  other arithmetic  2.66 us (3%)
    pallas_call x3, Pallas kernels, comm_call(): pl.pallas_call(kernel, out_shape=out_shape, in_specs=[pl.BlockSpec(memory...  49.5 us
    dot_general x1, matrix products, shards(): logits = jnp.dot(final, vocab_weight, preferred_element_type=jnp.float32)  15.6 us
    pallas_call x1, Pallas kernels, cached_attention(): pl.pallas_call(functools.partial(ragged_attention, block), out_shape=jax....  15.4 us
    unnamed x25, local copies, waits for them, and re-layouts  5.84 us
    dot_general x1, matrix products, shards(): jnp.dot(activation, down_weight, preferred_element_type=jnp.float32)  5.29 us
    dot_general x1, matrix products, shards(): jnp.dot(normed, query_weight, preferred_element_type=jnp.float32)  4.69 us

profile of v2, /device:TPU:0, one launch (start us, length us, event | category | flops | bytes accessed | tf_op | source)
XLA Modules:
  0.0 104.0 jit_solution(10931899501150055769)
XLA Ops:
  0.0 0.0 copy-start
  0.0 1.1 %fusion.9 = f32[8]{0:T(128)S(1)} fusion(bf16[8,4096]{1,0:T(8,128)(2,1)} %hidden_ref.1), kind=kLoop, calls=%fused_computation.18 | loop fusion | flops 98296 | bytes 65568 | tf_op jit(solution)/shard_map/reduce_sum | solution.py:22
  1.1 0.0 copy-start.6
  1.2 0.0 copy-start.3
  1.2 0.0 copy-start.9
  1.2 4.7 %convolution_bitcast_fusion = f32[1,8,8,128]{3,1,2,0:T(8,128)S(1)} fusion(bf16[4096,1024]{1,0:T(8,128)(2,1)} %param.19, bf16[8,4096]{1,0:T(8,128)(2,1)} %hidden_ref.1, f32[4096]{0:T(1024)} %param.18, f32[8]{0:T(128)S(1)} %add_rsqrt_fusion), kind=kOutput, calls=%fused_computation.5 | convolution fusion | flops 67239936 | bytes 8503328 | tf_op jit(solution)/shard_map/dot_general | solution.py:404
  5.9 0.0 copy-done.6
  5.9 0.1 multiply_cosine_fusion
  6.0 0.1 subtract_convert_fusion
  6.1 0.1 maximum_convert_fusion.query_ref
  6.2 0.0 copy-done
  6.2 0.0 copy-done.3
  6.2 0.0 copy-done.9
  6.2 0.4 fusion.22
  6.7 0.1 subtract_convert_fusion.1
  6.8 0.1 maximum_convert_fusion.1.key_ref
  6.8 2.0 %fusion.2 = f32[8,256]{1,0:T(8,128)S(1)} fusion(bf16[4096,256]{1,0:T(8,128)(2,1)} %param.21, bf16[8,4096]{1,0:T(8,128)(2,1)S(1)} %copy-done.3, f32[4096]{0:T(1024)S(1)} %copy-done.9, f32[8]{0:T(128)S(1)} %add_rsqrt_fusion), kind=kOutput, calls=%fused_computation.7 | convolution fusion | flops 16912384 | bytes 2187296 | tf_op jit(solution)/shard_map/dot_general | solution.py:413
  8.9 0.0 copy-start.2
  8.9 5.8 %copy-done.2 = bf16[8,2,4096,128]{3,2,1,0:T(8,128)(2,1)S(1)} copy-done((bf16[8,2,4096,128]{3,2,1,0:T(8,128)(2,1)S(1)}, bf16[8,2,4096,128]{3,2,1,0:T(8,128)(2,1)}, u32[]{:S(2)}) %copy-start.2) | copy-done | bytes 16777240
  14.6 0.0 copy-start.7
  14.6 15.4 %shard_map.163 = bf16[8,8,128]{2,1,0:T(8,128)(2,1)S(1)} custom-call(s32[8]{0:T(128)S(1)} %copy-done.6, f32[8,8,128]{2,1,0:T(8,128)S(1)} %maximum_convert_fusion.query_ref, f32[8,2,128]{2,1,0:T(2,128)S(1)} %maximum_convert_fusion.1.key_ref, f32[8,2,128]{2,1,0:T(2,128)S(1)} %reshape.98.value_ref, bf16[8,2,4096,128]{3,2,1,0:T(8,128)(2,1)S(1)} %copy-done.2, ...), custom_call_target="tpu_custom_call" | custom-call | tf_op jit(solution)/shard_map/pallas_call | solution.py:355
  30.1 0.0 copy-done.7
  30.1 0.0 copy-start.5
  30.1 0.0 copy-start.8
  30.1 1.2 %convolution_convert_fusion.1.partial_ref = bf16[8,4096]{1,0:T(8,128)(2,1)S(1)} fusion(bf16[1024,4096]{1,0:T(8,128)(2,1)S(1)} %copy-done.7, bf16[1,8,8,128]{3,2,1,0:T(8,128)(2,1)S(1)} %bitcast.37), kind=kOutput, calls=%fused_computation.2 | convolution fusion | flops 67141632 | bytes 8470528 | tf_op jit(solution)/shard_map/dot_general | solution.py:420
  31.3 0.0 copy-done.5
  31.3 16.4 %shard_map.164 = (bf16[8,8,4096]{2,1,0:T(8,128)(2,1)S(1)}, bf16[8,4096]{1,0:T(8,128)(2,1)S(1)}) custom-call(bf16[8,4096]{1,0:T(8,128)(2,1)S(1)} %convolution_convert_fusion.1.partial_ref, bf16[8,4096]{1,0:T(8,128)(2,1)S(1)} %copy-done.3, f32[1,4096]{1,0:T(1,128)S(1)} %bitcast.39), custom_call_target="tpu_custom_call" | custom-call | tf_op jit(solution)/shard_map/pallas_call | solution.py:230
  47.8 0.0 copy-done.8
  47.8 1.2 %fusion.7 = f32[64,448]{1,0:T(8,128)S(1)} fusion(bf16[4096,448]{0,1:T(8,128)(2,1)S(1)} %copy-done.8, bf16[8,8,4096]{2,1,0:T(8,128)(2,1)S(1)} %get-tuple-element.7), kind=kOutput, calls=%fused_computation.14 | convolution fusion | flops 234881024 | bytes 4308992 | tf_op jit(solution)/shard_map/dot_general | solution.py:438
  48.9 0.0 copy-start.4
  48.9 5.3 %fusion.partial_ref = bf16[8,8,4096]{2,1,0:T(8,128)(2,1)S(1)} fusion(bf16[448,4096]{1,0:T(8,128)(2,1)} %param.30, bf16[4096,448]{0,1:T(8,128)(2,1)} %param.29, bf16[8,8,4096]{2,1,0:T(8,128)(2,1)S(1)} %get-tuple-element.7, f32[64,448]{1,0:T(8,128)S(1)} %fusion.7), kind=kOutput, calls=%fused_computation.1 | convolution fusion | flops 470196224 | bytes 8503296 | tf_op jit(solution)/shard_map/dot_general | solution.py:441
  54.2 0.0 copy-done.4
  54.3 22.1 %shard_map.165 = bf16[8,8,4096]{2,1,0:T(8,128)(2,1)S(1)} custom-call(bf16[8,8,4096]{2,1,0:T(8,128)(2,1)S(1)} %fusion.partial_ref, bf16[8,4096]{1,0:T(8,128)(2,1)S(1)} %get-tuple-element.8.mixed_ref, f32[1,4096]{1,0:T(1,128)S(1)} %bitcast.38), custom_call_target="tpu_custom_call" | custom-call | tf_op jit(solution)/shard_map/pallas_call | solution.py:230
  76.3 0.0 copy-start.11
  76.3 0.0 copy-start.10
  76.3 0.0 copy-start.1
  76.4 15.6 %fusion.25 = (f32[64]{0:T(128)S(1)}, f32[64,4008]{1,0:T(8,128)S(1)}) fusion(bf16[4096,4008]{0,1:T(8,128)(2,1)} %param.32, bf16[8,8,4096]{2,1,0:T(8,128)(2,1)S(1)} %shard_map.165), kind=kOutput, calls=%fused_computation.48 | convolution fusion | flops 2101602816 | bytes 34384128 | tf_op jit(solution)/shard_map/dot_general | solution.py:461
  92.0 0.0 copy-done.11
  92.0 0.5 exponential_reduce_fusion
  92.5 11.0 %shard_map.166 = f32[8,128]{1,0:T(8,128)S(1)} custom-call(f32[8,128]{1,0:T(8,128)S(1)} %select_maximum_fusion.stats_ref), custom_call_target="tpu_custom_call" | custom-call | tf_op jit(solution)/shard_map/pallas_call | solution.py:230
  103.4 0.0 copy-done.10
  103.5 0.6 compare_select_fusion
  104.0 0.0 copy-done.1
  (9 shorter events, 0.1 us)
Async XLA Ops:
  0.0 6.2 %copy-start = (bf16[4096,256]{1,0:T(8,128)(2,1)S(1)}, bf16[4096,256]{1,0:T(8,128)(2,1)}, u32[]{:S(2)}) copy-start(bf16[4096,256]{1,0:T(8,128)(2,1)} %param.20) | copy-start | bytes 6291460
  1.1 4.7 %copy-start.6 = (s32[8]{0:T(128)S(1)}, s32[8]{0:T(128)}, u32[]{:S(2)}) copy-start(s32[8]{0:T(128)} %lengths_ref.1) | copy-start | bytes 100
  1.2 5.1 %copy-start.3 = (bf16[8,4096]{1,0:T(8,128)(2,1)S(1)}, bf16[8,4096]{1,0:T(8,128)(2,1)}, u32[]{:S(2)}) copy-start(bf16[8,4096]{1,0:T(8,128)(2,1)} %hidden_ref.1) | copy-start | bytes 196612
  1.2 5.1 %copy-start.9 = (f32[4096]{0:T(1024)S(1)}, f32[4096]{0:T(1024)}, u32[]{:S(2)}) copy-start(f32[4096]{0:T(1024)} %param.18) | copy-start | bytes 49156
  8.9 5.8 %copy-start.2 = (bf16[8,2,4096,128]{3,2,1,0:T(8,128)(2,1)S(1)}, bf16[8,2,4096,128]{3,2,1,0:T(8,128)(2,1)}, u32[]{:S(2)}) copy-start(bf16[8,2,4096,128]{3,2,1,0:T(8,128)(2,1)} %key_hbm.1) | copy-start | bytes 50331652
  14.6 15.5 %copy-start.7 = (bf16[1024,4096]{1,0:T(8,128)(2,1)S(1)}, bf16[1024,4096]{1,0:T(8,128)(2,1)}, u32[]{:S(2)}) copy-start(bf16[1024,4096]{1,0:T(8,128)(2,1)} %param.22) | copy-start | bytes 25165828
  30.1 1.2 %copy-start.5 = (f32[4096]{0:T(1024)S(1)}, f32[4096]{0:T(1024)}, u32[]{:S(2)}) copy-start(f32[4096]{0:T(1024)} %param.27) | copy-start | bytes 49156
  30.1 17.6 %copy-start.8 = (bf16[4096,448]{0,1:T(8,128)(2,1)S(1)}, bf16[4096,448]{0,1:T(8,128)(2,1)}, u32[]{:S(2)}) copy-start(bf16[4096,448]{0,1:T(8,128)(2,1)} %param.28) | copy-start | bytes 11010052
  48.9 5.3 %copy-start.4 = (f32[4096]{0:T(1024)S(1)}, f32[4096]{0:T(1024)}, u32[]{:S(2)}) copy-start(f32[4096]{0:T(1024)} %param.31) | copy-start | bytes 49156
  76.3 15.6 %copy-start.11 = (s32[64]{0:T(128)S(1)}, s32[64]{0:T(128)}, u32[]{:S(2)}) copy-start(s32[64]{0:T(128)} %param.33) | copy-start | bytes 772
  76.3 27.1 %copy-start.10 = (s32[8]{0:T(128)S(1)}, s32[8]{0:T(128)}, u32[]{:S(2)}) copy-start(s32[8]{0:T(128)} %param.26) | copy-start | bytes 100
  76.3 27.7 %copy-start.1 = (bf16[4096,256]{1,0:T(8,128)(2,1)S(1)}, bf16[4096,256]{1,0:T(8,128)(2,1)}, u32[]{:S(2)}) copy-start(bf16[4096,256]{1,0:T(8,128)(2,1)} %param.20) | copy-start | bytes 6291460

commit v3 on v2

--- a/solution.py
+++ b/solution.py
@@ -351,7 +351,7 @@
     block = math.gcd(places, 2048)
     buffers = VMEM((3, key_heads, block, width), jnp.bfloat16)
     whole = pl.BlockSpec(memory_space=VMEM)
-    away = pl.BlockSpec(memory_space=pl.ANY)
+    away = pl.BlockSpec(memory_space=pltpu.HBM)
     return pl.pallas_call(
         functools.partial(ragged_attention, block),
         out_shape=jax.ShapeDtypeStruct((rollouts, heads, width), jnp.bfloat16),
@@ -366,7 +366,10 @@
             VMEM((heads, 128), jnp.float32),
             VMEM((heads, width), jnp.float32),
         ],
-        compiler_params=pltpu.CompilerParams(vmem_limit_bytes=24 * 1024 * 1024),
+        compiler_params=pltpu.CompilerParams(vmem_limit_bytes=50 * 1024 * 1024),
+        cost_estimate=pl.CostEstimate(
+            flops=10_000_000_000, bytes_accessed=20_000_000, transcendentals=0
+        ),
     )(
         lengths,
         queries.astype(jnp.float32),

time: 104 us -> 102 us (0.981); the launches traced: 104 us -> 100 us
  local copies, waits for them, and re-layouts: 5.87 us -> 0.1 us
  matrix products: 30.4 us -> 33.9 us
  Pallas kernels: 64.9 us -> 63.3 us
    pallas_call x1, Pallas kernels: 15.4 us -> 9.59 us  [cached_attention(): pl.pallas_call(functools.partial(ragged_attention, block), out_shape=jax....]
    unnamed x25 -> x21, local copies, waits for them, and re-layouts: 5.84 us -> 0.07 us
    pallas_call x3, Pallas kernels: 49.5 us -> 53.8 us  [comm_call(): pl.pallas_call(kernel, out_shape=out_shape, in_specs=[pl.BlockSpec(memory...]
    dot_general x1, matrix products: 1.19 us -> 4.72 us  [shards(): jnp.dot(attended.reshape(local_rows, key_heads * groups * head_width), ou...]
where the time goes in v3:
time: 102 us; the launch traced here: 100 us
  Pallas kernels  63.3 us (62%)
  matrix products  33.9 us (33%)
  other arithmetic  2.66 us (3%)
    pallas_call x3, Pallas kernels, comm_call(): pl.pallas_call(kernel, out_shape=out_shape, in_specs=[pl.BlockSpec(memory...  53.8 us
    dot_general x1, matrix products, shards(): logits = jnp.dot(final, vocab_weight, preferred_element_type=jnp.float32)  15.6 us
    pallas_call x1, Pallas kernels, cached_attention(): pl.pallas_call(functools.partial(ragged_attention, block), out_shape=jax....  9.59 us
    dot_general x1, matrix products, shards(): jnp.dot(activation, down_weight, preferred_element_type=jnp.float32)  5.29 us
    dot_general x1, matrix products, shards(): jnp.dot(attended.reshape(local_rows, key_heads * groups * head_width), ou...  4.72 us
    dot_general x1, matrix products, shards(): jnp.dot(normed, query_weight, preferred_element_type=jnp.float32)  4.69 us

profile of v3, /device:TPU:0, one launch (start us, length us, event | category | flops | bytes accessed | tf_op | source)
XLA Modules:
  0.0 100.2 jit_solution(18416792460742970807)
XLA Ops:
  0.0 0.0 copy-start
  0.0 1.1 %fusion.9 = f32[8]{0:T(128)S(1)} fusion(bf16[8,4096]{1,0:T(8,128)(2,1)} %hidden_ref.1), kind=kLoop, calls=%fused_computation.18 | loop fusion | flops 98296 | bytes 65568 | tf_op jit(solution)/shard_map/reduce_sum | solution.py:22
  1.1 0.0 copy-start.5
  1.2 0.0 copy-start.2
  1.2 0.0 copy-start.7
  1.2 4.7 %convolution_bitcast_fusion = f32[1,8,8,128]{3,1,2,0:T(8,128)S(1)} fusion(bf16[4096,1024]{1,0:T(8,128)(2,1)} %param.19, bf16[8,4096]{1,0:T(8,128)(2,1)} %hidden_ref.1, f32[4096]{0:T(1024)} %param.18, f32[8]{0:T(128)S(1)} %add_rsqrt_fusion), kind=kOutput, calls=%fused_computation.5 | convolution fusion | flops 67239936 | bytes 8503328 | tf_op jit(solution)/shard_map/dot_general | solution.py:407
  5.9 0.0 copy-done.5
  5.9 0.1 multiply_cosine_fusion
  6.0 0.1 subtract_convert_fusion
  6.1 0.1 maximum_convert_fusion.query_ref
  6.2 0.0 copy-done
  6.2 0.0 copy-done.2
  6.2 0.0 copy-done.7
  6.2 0.4 fusion.22
  6.7 0.1 subtract_convert_fusion.1
  6.8 0.1 maximum_convert_fusion.1.key_ref
  6.8 2.0 %fusion.2 = f32[8,256]{1,0:T(8,128)S(1)} fusion(bf16[4096,256]{1,0:T(8,128)(2,1)} %param.21, bf16[8,4096]{1,0:T(8,128)(2,1)S(1)} %copy-done.2, f32[4096]{0:T(1024)S(1)} %copy-done.7, f32[8]{0:T(128)S(1)} %add_rsqrt_fusion), kind=kOutput, calls=%fused_computation.7 | convolution fusion | flops 16912384 | bytes 2187296 | tf_op jit(solution)/shard_map/dot_general | solution.py:416
  8.9 9.6 %shard_map.163 = bf16[8,8,128]{2,1,0:T(8,128)(2,1)S(1)} custom-call(s32[8]{0:T(128)S(1)} %copy-done.5, f32[8,8,128]{2,1,0:T(8,128)S(1)} %maximum_convert_fusion.query_ref, f32[8,2,128]{2,1,0:T(2,128)S(1)} %maximum_convert_fusion.1.key_ref, f32[8,2,128]{2,1,0:T(2,128)S(1)} %reshape.98.value_ref, bf16[8,2,4096,128]{3,2,1,0:T(8,128)(2,1)} %key_hbm.1, ...), custom_call_target="tpu_custom_call" | custom-call | flops 10000000000 | bytes 20000000 | tf_op jit(solution)/shard_map/pallas_call | solution.py:355
  18.4 0.0 copy-start.4
  18.5 0.0 copy-start.6
  18.5 4.7 %convolution_convert_fusion.1.partial_ref = bf16[8,4096]{1,0:T(8,128)(2,1)S(1)} fusion(bf16[1024,4096]{1,0:T(8,128)(2,1)} %param.22, bf16[1,8,8,128]{3,2,1,0:T(8,128)(2,1)S(1)} %bitcast.37), kind=kOutput, calls=%fused_computation.2 | convolution fusion | flops 67141632 | bytes 8470528 | tf_op jit(solution)/shard_map/dot_general | solution.py:423
  23.2 0.0 copy-done.4
  23.2 20.6 %shard_map.164 = (bf16[8,8,4096]{2,1,0:T(8,128)(2,1)S(1)}, bf16[8,4096]{1,0:T(8,128)(2,1)S(1)}) custom-call(bf16[8,4096]{1,0:T(8,128)(2,1)S(1)} %convolution_convert_fusion.1.partial_ref, bf16[8,4096]{1,0:T(8,128)(2,1)S(1)} %copy-done.2, f32[1,4096]{1,0:T(1,128)S(1)} %bitcast.39), custom_call_target="tpu_custom_call" | custom-call | tf_op jit(solution)/shard_map/pallas_call | solution.py:230
  43.9 0.0 copy-done.6
  43.9 1.2 %fusion.7 = f32[64,448]{1,0:T(8,128)S(1)} fusion(bf16[4096,448]{0,1:T(8,128)(2,1)S(1)} %copy-done.6, bf16[8,8,4096]{2,1,0:T(8,128)(2,1)S(1)} %get-tuple-element.7), kind=kOutput, calls=%fused_computation.14 | convolution fusion | flops 234881024 | bytes 4308992 | tf_op jit(solution)/shard_map/dot_general | solution.py:441
  45.0 0.0 copy-start.3
  45.0 5.3 %fusion.partial_ref = bf16[8,8,4096]{2,1,0:T(8,128)(2,1)S(1)} fusion(bf16[448,4096]{1,0:T(8,128)(2,1)} %param.30, bf16[4096,448]{0,1:T(8,128)(2,1)} %param.29, bf16[8,8,4096]{2,1,0:T(8,128)(2,1)S(1)} %get-tuple-element.7, f32[64,448]{1,0:T(8,128)S(1)} %fusion.7), kind=kOutput, calls=%fused_computation.1 | convolution fusion | flops 470196224 | bytes 8503296 | tf_op jit(solution)/shard_map/dot_general | solution.py:444
  50.3 0.0 copy-done.3
  50.4 22.2 %shard_map.165 = bf16[8,8,4096]{2,1,0:T(8,128)(2,1)S(1)} custom-call(bf16[8,8,4096]{2,1,0:T(8,128)(2,1)S(1)} %fusion.partial_ref, bf16[8,4096]{1,0:T(8,128)(2,1)S(1)} %get-tuple-element.8.mixed_ref, f32[1,4096]{1,0:T(1,128)S(1)} %bitcast.38), custom_call_target="tpu_custom_call" | custom-call | tf_op jit(solution)/shard_map/pallas_call | solution.py:230
  72.5 0.0 copy-start.9
  72.6 0.0 copy-start.8
  72.6 0.0 copy-start.1
  72.6 15.6 %fusion.25 = (f32[64]{0:T(128)S(1)}, f32[64,4008]{1,0:T(8,128)S(1)}) fusion(bf16[4096,4008]{0,1:T(8,128)(2,1)} %param.32, bf16[8,8,4096]{2,1,0:T(8,128)(2,1)S(1)} %shard_map.165), kind=kOutput, calls=%fused_computation.48 | convolution fusion | flops 2101602816 | bytes 34384128 | tf_op jit(solution)/shard_map/dot_general | solution.py:464
  88.2 0.0 copy-done.9
  88.2 0.5 exponential_reduce_fusion
  88.7 10.9 %shard_map.166 = f32[8,128]{1,0:T(8,128)S(1)} custom-call(f32[8,128]{1,0:T(8,128)S(1)} %select_maximum_fusion.stats_ref), custom_call_target="tpu_custom_call" | custom-call | tf_op jit(solution)/shard_map/pallas_call | solution.py:230
  99.6 0.0 copy-done.8
  99.6 0.6 compare_select_fusion
  100.2 0.0 copy-done.1
  (9 shorter events, 0.1 us)
Async XLA Ops:
  0.0 6.2 %copy-start = (bf16[4096,256]{1,0:T(8,128)(2,1)S(1)}, bf16[4096,256]{1,0:T(8,128)(2,1)}, u32[]{:S(2)}) copy-start(bf16[4096,256]{1,0:T(8,128)(2,1)} %param.20) | copy-start | bytes 6291460
  1.1 4.7 %copy-start.5 = (s32[8]{0:T(128)S(1)}, s32[8]{0:T(128)}, u32[]{:S(2)}) copy-start(s32[8]{0:T(128)} %lengths_ref.1) | copy-start | bytes 100
  1.2 5.1 %copy-start.2 = (bf16[8,4096]{1,0:T(8,128)(2,1)S(1)}, bf16[8,4096]{1,0:T(8,128)(2,1)}, u32[]{:S(2)}) copy-start(bf16[8,4096]{1,0:T(8,128)(2,1)} %hidden_ref.1) | copy-start | bytes 196612
  1.2 5.1 %copy-start.7 = (f32[4096]{0:T(1024)S(1)}, f32[4096]{0:T(1024)}, u32[]{:S(2)}) copy-start(f32[4096]{0:T(1024)} %param.18) | copy-start | bytes 49156
  18.4 4.8 %copy-start.4 = (f32[4096]{0:T(1024)S(1)}, f32[4096]{0:T(1024)}, u32[]{:S(2)}) copy-start(f32[4096]{0:T(1024)} %param.27) | copy-start | bytes 49156
  18.5 25.4 %copy-start.6 = (bf16[4096,448]{0,1:T(8,128)(2,1)S(1)}, bf16[4096,448]{0,1:T(8,128)(2,1)}, u32[]{:S(2)}) copy-start(bf16[4096,448]{0,1:T(8,128)(2,1)} %param.28) | copy-start | bytes 11010052
  45.0 5.3 %copy-start.3 = (f32[4096]{0:T(1024)S(1)}, f32[4096]{0:T(1024)}, u32[]{:S(2)}) copy-start(f32[4096]{0:T(1024)} %param.31) | copy-start | bytes 49156
  72.5 15.6 %copy-start.9 = (s32[64]{0:T(128)S(1)}, s32[64]{0:T(128)}, u32[]{:S(2)}) copy-start(s32[64]{0:T(128)} %param.33) | copy-start | bytes 772
  72.6 27.1 %copy-start.8 = (s32[8]{0:T(128)S(1)}, s32[8]{0:T(128)}, u32[]{:S(2)}) copy-start(s32[8]{0:T(128)} %param.26) | copy-start | bytes 100
  72.6 27.7 %copy-start.1 = (bf16[4096,256]{1,0:T(8,128)(2,1)S(1)}, bf16[4096,256]{1,0:T(8,128)(2,1)}, u32[]{:S(2)}) copy-start(bf16[4096,256]{1,0:T(8,128)(2,1)} %param.20) | copy-start | bytes 6291460
